TPU v7x, 256 devices: a 2x2x32 block of a 4x8x32 slice. The times are simulated.
256 devices in a mesh: groups: 4 (over x, y), seq: 64 (over z, core).
Axes of the slice: x: 2, y: 2, z: 32, core: 2. Of those that a mesh axis runs over, the one named last changes fastest.
The devices are a block of a 4x8x32 slice.
Arguments:
- video_qkv: bfloat16 [16, 16, 3, 3072, 128], P('groups', None, None, 'seq'), parts along dimension 0, may hold values from -9 to 9
- video_cross: bfloat16 [16, 16, 3, 3072, 128], P('groups', None, None, 'seq'), parts along dimension 0, may hold values from -9 to 9
- audio_qkv: bfloat16 [16, 16, 3, 768, 128], P('groups', None, None, 'seq'), parts along dimension 0, may hold values from -9 to 9
- audio_cross: bfloat16 [16, 16, 3, 768, 128], P('groups', None, None, 'seq'), parts along dimension 0, may hold values from -9 to 9
- lengths: int32 [2, 16], P(None, 'groups'), parts along dimension 1, may hold values from 384 to 3072, as said below
- timestep: int32 [4], P('groups'), parts along dimension 0, may hold values from 0 to 49
- gate_table: float32 [50, 4, 16, 128], replicated, may hold values from -4 to 4
Outputs:
- video_out: bfloat16 [16, 16, 3072, 128], P('groups', None, 'seq'), parts along dimension 0
- audio_out: bfloat16 [16, 16, 768, 128], P('groups', None, 'seq'), parts along dimension 0
There are 4 independent parts, one for each index of `groups`. A program takes and returns all parts, laid end to end along the dimension named above; an argument that names none is the same for every part. Nothing has to cross between parts.
Inputs may be any that keep to these rules, and one draw needn't show every extreme that they name: `lengths`: row 0 holds each clip's valid video token count, row 1 its valid audio token count; every count is at least half of its tower's length (3072 or 768), and in every draw some clip has all 3072 video tokens and some clip all 768 audio tokens valid.
All inputs are finite; a program needn't handle non-finite values.
Results may differ from a plain program's by a relative error of at most 0.0085.
Values may be sent and summed in bfloat16 or wider, within the bound.
A program may use at most 64 MiB of HBM per device.

v0:
```python
import math

import jax
import jax.numpy as jnp
from jax import lax
from jax.sharding import Mesh
from jax.sharding import PartitionSpec as P

SEQ = ("seq_0", "seq_1")


def split_up(value, dim, devices):
    shape = value.shape
    pieces = value.reshape(*shape[:dim], devices, shape[dim] // devices, *shape[dim + 1 :])
    return jnp.moveaxis(pieces, dim, 0)


def joined_along(pieces, dim):
    shape = list(pieces.shape[1:])
    shape[dim] *= pieces.shape[0]
    return jnp.moveaxis(pieces, 0, dim).reshape(shape)


def exchange_in_order(pieces, axes, order):
    inside = pieces.shape[1:]
    out = pieces.reshape(*(lax.axis_size(a) for a in axes), *inside)
    for k in order:
        out = lax.all_to_all(out, axes[k], k, k, tiled=True)
    return out.reshape(-1, *inside)


def two_step_exchange(value, groups, order, split_dim, concat_dim):
    devices = lax.axis_size(groups[0]) * lax.axis_size(groups[1])
    pieces = split_up(value, split_dim, devices)
    return joined_along(exchange_in_order(pieces, groups, order), concat_dim)


def attend(queries, key_rows, values, keep_len):
    row_count = queries.shape[0]
    block_rows = row_count if row_count <= 1024 else math.gcd(row_count, 1024)
    score_scale = 1.0 / math.sqrt(queries.shape[1])
    columns = jnp.arange(key_rows.shape[0], dtype=jnp.int32)
    visible = columns[None, :] < keep_len
    blocks = queries.reshape(row_count // block_rows, block_rows, queries.shape[1])

    def one_block(query_block):
        scores = (
            lax.dot_general(
                query_block, key_rows, (((1,), (1,)), ((), ())), preferred_element_type=jnp.float32
            )
            * score_scale
        )
        scores = jnp.where(visible, scores, -1e30)
        row_max = jnp.max(scores, axis=1, keepdims=True)
        weights = jnp.exp(scores - row_max)
        row_total = jnp.sum(weights, axis=1, keepdims=True)
        shares = (weights / row_total).astype(jnp.bfloat16)
        return jnp.dot(shares, values, preferred_element_type=jnp.float32).astype(jnp.bfloat16)

    return lax.map(one_block, blocks).reshape(row_count, queries.shape[1])


def pair_outputs(bundle):
    video_set, video_far, audio_set, audio_far, video_len, audio_len = bundle
    self_video = attend(video_set[0], video_set[1], video_set[2], video_len)
    cross_video = attend(video_far[0], audio_far[1], audio_far[2], audio_len)
    self_audio = attend(audio_set[0], audio_set[1], audio_set[2], audio_len)
    cross_audio = attend(audio_far[0], video_far[1], video_far[2], video_len)
    return (self_video, cross_video, self_audio, cross_audio)


def mix_pairs(self_part, cross_part, gate_self, gate_cross):
    mixed_sum = gate_self[:, None, :] * self_part.astype(jnp.float32) + gate_cross[
        :, None, :
    ] * cross_part.astype(jnp.float32)
    return mixed_sum.astype(jnp.bfloat16)


def on_device(video_qkv, video_cross, audio_qkv, audio_cross, lengths, timestep, gate_table):
    group_size = lax.axis_size(SEQ)
    clip_count, head_count = (video_qkv.shape[0], video_qkv.shape[1])
    video_rows, audio_rows, head_size = (video_qkv.shape[3], audio_qkv.shape[3], video_qkv.shape[4])
    pair_count = clip_count * head_count
    pair_local = pair_count // group_size

    def to_pairs(tensor):
        return tensor.reshape((pair_count,) + tensor.shape[2:])

    joined_set = jnp.concatenate([to_pairs(video_qkv), to_pairs(audio_qkv)], axis=2)
    joined_far = jnp.concatenate([to_pairs(video_cross), to_pairs(audio_cross)], axis=2)
    arrived_set, arrived_far = (
        lax.all_to_all(joined_set, SEQ, split_axis=0, concat_axis=2, tiled=True),
        lax.all_to_all(joined_far, SEQ, split_axis=0, concat_axis=2, tiled=True),
    )

    def split_towers(arrived):
        blocked = arrived.reshape(pair_local, 3, group_size, video_rows + audio_rows, head_size)
        video_part = blocked[:, :, :, :video_rows].reshape(
            pair_local, 3, group_size * video_rows, head_size
        )
        audio_part = blocked[:, :, :, video_rows:].reshape(
            pair_local, 3, group_size * audio_rows, head_size
        )
        return (video_part, audio_part)

    video_set, audio_set = split_towers(arrived_set)
    video_far, audio_far = split_towers(arrived_far)
    pair_ids = lax.axis_index(SEQ) * pair_local + jnp.arange(pair_local, dtype=jnp.int32)
    clip_hot = (pair_ids // head_count)[:, None] == jnp.arange(clip_count, dtype=jnp.int32)[None, :]
    video_lens = jnp.sum(jnp.where(clip_hot, lengths[0][None, :], 0), axis=1)
    audio_lens = jnp.sum(jnp.where(clip_hot, lengths[1][None, :], 0), axis=1)
    self_video, cross_video, self_audio, cross_audio = lax.map(
        pair_outputs, (video_set, video_far, audio_set, audio_far, video_lens, audio_lens)
    )
    step_ids = jnp.arange(gate_table.shape[0], dtype=jnp.int32)
    gate_rows = jnp.sum(
        jnp.where((step_ids == timestep[0])[:, None, None, None], gate_table, 0.0), axis=0
    )
    head_hot = (pair_ids % head_count)[:, None] == jnp.arange(head_count, dtype=jnp.int32)[None, :]
    pair_gates = jnp.sum(
        jnp.where(head_hot[None, :, :, None], gate_rows[:, None, :, :], 0.0), axis=2
    )
    mix_video = mix_pairs(self_video, cross_video, pair_gates[0], pair_gates[1])
    mix_audio = mix_pairs(self_audio, cross_audio, pair_gates[2], pair_gates[3])
    video_out = two_step_exchange(mix_video, ("seq_0", "seq_1"), (1, 0), 1, 0).reshape(
        clip_count, head_count, video_rows, head_size
    )
    audio_out = two_step_exchange(mix_audio, ("seq_0", "seq_1"), (1, 0), 1, 0).reshape(
        clip_count, head_count, audio_rows, head_size
    )
    return (video_out, audio_out)


def solution(mesh):
    split = Mesh(mesh.devices.reshape(mesh.shape["groups"], 32, 2), ("groups", "seq_0", "seq_1"))
    return jax.shard_map(
        on_device,
        mesh=split,
        in_specs=(
            P("groups", None, None, SEQ, None),
            P("groups", None, None, SEQ, None),
            P("groups", None, None, SEQ, None),
            P("groups", None, None, SEQ, None),
            P(None, "groups"),
            P("groups"),
            P(),
        ),
        out_specs=(P("groups", None, SEQ, None), P("groups", None, SEQ, None)),
        check_vma=False,
    )
```

profile of v0, /device:TPU:37, one launch (start us, length us, event | category | flops | bytes accessed | tf_op | source)
XLA Modules:
  0.0 827.3 jit_solution(11493166511218997875)
XLA Ops:
  2.5 2.6 pad_maximum_fusion.1
  5.1 34.3 %all-to-all-start.1 = ((bf16[64,3,60,128]{3,2,1,0:T(8,128)(2,1)}), bf16[64,3,60,128]{3,2,1,0:T(8,128)(2,1)S(1)}, u32[]{:S(2)}, u32[]{:S(2)}) async-start(bf16[64,3,60,128]{3,2,1,0:T(8,128)(2,1)} %pad_maximum_fusion.1), calls=%async_computation.1 | async-start | bytes 6291456 | tf_op jit(solution)/shard_map/all_to_all | solution.py:93
  41.3 2.7 pad_maximum_fusion
  44.0 279.4 %all-to-all-done.1 = bf16[64,3,60,128]{3,2,1,0:T(8,128)(2,1)S(1)} async-done(((bf16[64,3,60,128]{3,2,1,0:T(8,128)(2,1)}), bf16[64,3,60,128]{3,2,1,0:T(8,128)(2,1)S(1)}, u32[]{:S(2)}, u32[]{:S(2)}) %all-to-all-start.1) | async-done | bytes 2949152 | tf_op jit(solution)/shard_map/all_to_all | solution.py:93
  323.4 12.0 %all-to-all-start = ((bf16[64,3,60,128]{3,2,1,0:T(8,128)(2,1)}), bf16[64,3,60,128]{3,2,1,0:T(8,128)(2,1)}, u32[]{:S(2)}, u32[]{:S(2)}) async-start(bf16[64,3,60,128]{3,2,1,0:T(8,128)(2,1)} %pad_maximum_fusion), calls=%async_computation | async-start | bytes 6291456 | tf_op jit(solution)/shard_map/all_to_all | solution.py:92
  337.8 1.6 select_reduce_fusion
  342.5 279.1 %all-to-all-done = bf16[64,3,60,128]{3,2,1,0:T(8,128)(2,1)} async-done(((bf16[64,3,60,128]{3,2,1,0:T(8,128)(2,1)}), bf16[64,3,60,128]{3,2,1,0:T(8,128)(2,1)}, u32[]{:S(2)}, u32[]{:S(2)}) %all-to-all-start) | async-done | bytes 2949152 | tf_op jit(solution)/shard_map/all_to_all | solution.py:92
  621.7 2.0 fusion.50
  623.7 3.0 fusion.53
  627.8 1.7 fusion.28
  629.5 2.1 fusion.29
  632.7 2.2 fusion.43
  636.7 8.4 %all-to-all-start.4 = ((bf16[32,2,1,12,128]{4,0,3,2,1:T(8,128)(2,1)}), bf16[32,2,1,12,128]{4,0,3,2,1:T(8,128)(2,1)}, u32[]{:S(2)}, u32[]{:S(2)}) async-start(bf16[32,2,1,12,128]{4,0,3,2,1:T(8,128)(2,1)} %copy.44), calls=%async_computation.4 | async-start | bytes 393216 | tf_op jit(solution)/shard_map/all_to_all | solution.py:28
  645.3 29.8 %while.47 = (s32[]{:T(128)}, bf16[3,1024,128]{2,1,0:T(8,128)(2,1)S(1)}, bf16[3,1024,128]{2,1,0:T(8,128)(2,1)S(1)}, bf16[3072,128]{1,0:T(8,128)(2,1)S(1)}, bf16[3072,128]{1,0:T(8,128)(2,1)}, /*index=5*/s32[]{:T(128)}, s32[]{:T(128)}) while((s32[]{:T(128)}, bf16[3,1024,128]{2,1,0:T(8,128)(2,1)S(1)}, ...), condition=%wide.region_6.7_spmd.clone, body=%wide.region_3.6_spmd.clone.sunk | while | flops 1648493568 | bytes 43024500 | solution.py:60
  645.9 2.1 fusion.76
  648.1 2.7 fusion.77
  650.8 4.4 fusion.78
  655.9 2.1 fusion.76
  658.0 2.7 fusion.77
  660.7 4.4 fusion.78
  665.8 2.1 fusion.76
  667.9 2.7 fusion.77
  670.7 4.4 fusion.78
  675.3 12.8 %while.48 = (s32[]{:T(128)}, bf16[3,1024,128]{2,1,0:T(8,128)(2,1)S(1)}, bf16[3,1024,128]{2,1,0:T(8,128)(2,1)}, bf16[768,128]{1,0:T(8,128)(2,1)S(1)}, bf16[768,128]{1,0:T(8,128)(2,1)S(1)}, /*index=5*/s32[]{:T(128)}, s32[]{:T(128)}) while((s32[]{:T(128)}, bf16[3,1024,128]{2,1,0:T(8,128)(2,1)S(1)}, ...), condition=%wide.region_11.12_spmd.clone, body=%wide.region_8.11_spmd.clone.sunk | while | flops 412220160 | bytes 10379093 | solution.py:60
  680.2 1.5 fusion.81
  684.5 1.5 fusion.81
  689.4 3.8 all-to-all-start.2
  693.2 1.8 copy.45
  695.0 4.8 all-to-all-start.5
  700.7 35.7 %all-to-all-done.5 = bf16[32,2,1,12,128]{4,1,3,2,0:T(2,128)(2,1)S(1)} async-done(((bf16[32,2,1,12,128]{4,1,3,2,0:T(2,128)(2,1)}), bf16[32,2,1,12,128]{4,1,3,2,0:T(2,128)(2,1)S(1)}, u32[]{:S(2)}, u32[]{:S(2)}) %all-to-all-start.5) | async-done | bytes 196640 | tf_op jit(solution)/shard_map/all_to_all | solution.py:28
  736.5 4.8 all-to-all-start.3
  742.2 84.3 %all-to-all-done.3 = bf16[32,2,1,48,128]{4,3,1,2,0:T(8,128)(2,1)S(1)} async-done(((bf16[32,2,1,48,128]{4,3,1,2,0:T(8,128)(2,1)}), bf16[32,2,1,48,128]{4,3,1,2,0:T(8,128)(2,1)S(1)}, u32[]{:S(2)}, u32[]{:S(2)}) %all-to-all-start.3) | async-done | bytes 786464 | tf_op jit(solution)/shard_map/all_to_all | solution.py:28
  (71 shorter events, 28.3 us)
Async XLA Ops:
  0.6 1.8 copy-start.1
  5.1 318.2 %all-to-all-start.1 = ((bf16[64,3,60,128]{3,2,1,0:T(8,128)(2,1)}), bf16[64,3,60,128]{3,2,1,0:T(8,128)(2,1)S(1)}, u32[]{:S(2)}, u32[]{:S(2)}) async-start(bf16[64,3,60,128]{3,2,1,0:T(8,128)(2,1)} %pad_maximum_fusion.1), calls=%async_computation.1 | async-start | bytes 6291456 | tf_op jit(solution)/shard_map/all_to_all | solution.py:93
  39.5 1.8 copy-start.2
  44.0 292.0 %copy-start.9 = (s32[2,4]{1,0:T(2,128)S(1)}, s32[2,4]{1,0:T(2,128)}, u32[]{:S(2)}) copy-start(s32[2,4]{1,0:T(2,128)} %param.15) | copy-start | bytes 100
  323.4 298.3 %all-to-all-start = ((bf16[64,3,60,128]{3,2,1,0:T(8,128)(2,1)}), bf16[64,3,60,128]{3,2,1,0:T(8,128)(2,1)}, u32[]{:S(2)}, u32[]{:S(2)}) async-start(bf16[64,3,60,128]{3,2,1,0:T(8,128)(2,1)} %pad_maximum_fusion), calls=%async_computation | async-start | bytes 6291456 | tf_op jit(solution)/shard_map/all_to_all | solution.py:92
  623.7 4.2 copy-start
  631.5 1.1 copy-start.6
  636.7 52.7 %all-to-all-start.4 = ((bf16[32,2,1,12,128]{4,0,3,2,1:T(8,128)(2,1)}), bf16[32,2,1,12,128]{4,0,3,2,1:T(8,128)(2,1)}, u32[]{:S(2)}, u32[]{:S(2)}) async-start(bf16[32,2,1,12,128]{4,0,3,2,1:T(8,128)(2,1)} %copy.44), calls=%async_computation.4 | async-start | bytes 393216 | tf_op jit(solution)/shard_map/all_to_all | solution.py:28
  645.3 29.8 %copy-start.4 = (bf16[1,1,64,12,128]{4,3,1,2,0:T(8,128)(2,1)S(1)}, bf16[1,1,64,12,128]{4,3,1,2,0:T(8,128)(2,1)}, u32[]{:S(2)}) copy-start(bf16[1,1,64,12,128]{4,3,1,2,0:T(8,128)(2,1)} %get-tuple-element.225) | copy-start | bytes 589828
  645.3 29.9 %copy-start.3 = (bf16[1,1,64,12,128]{4,3,1,2,0:T(8,128)(2,1)S(1)}, bf16[1,1,64,12,128]{4,3,1,2,0:T(8,128)(2,1)}, u32[]{:S(2)}) copy-start(bf16[1,1,64,12,128]{4,3,1,2,0:T(8,128)(2,1)} %get-tuple-element.224) | copy-start | bytes 589828
  648.1 2.7 copy-start.5
  658.0 2.7 copy-start.5
  667.9 2.7 copy-start.5
  675.3 12.8 %copy-start.7 = (f32[128]{0:T(128)S(1)}, f32[128]{0:T(128)}, u32[]{:S(2)}) copy-start(f32[128]{0:T(128)} %get-tuple-element.231) | copy-start | bytes 1540
  675.3 12.8 %copy-start.8 = (f32[128]{0:T(128)S(1)}, f32[128]{0:T(128)}, u32[]{:S(2)}) copy-start(f32[128]{0:T(128)} %get-tuple-element.232) | copy-start | bytes 1540
  689.4 5.6 all-to-all-start.2
  695.0 41.5 %all-to-all-start.5 = ((bf16[32,2,1,12,128]{4,1,3,2,0:T(2,128)(2,1)}), bf16[32,2,1,12,128]{4,1,3,2,0:T(2,128)(2,1)S(1)}, u32[]{:S(2)}, u32[]{:S(2)}) async-start(bf16[32,2,1,12,128]{4,1,3,2,0:T(2,128)(2,1)} %copy.45), calls=%async_computation.5 | async-start | bytes 393216 | tf_op jit(solution)/shard_map/all_to_all | solution.py:28
  736.5 90.0 %all-to-all-start.3 = ((bf16[32,2,1,48,128]{4,3,1,2,0:T(8,128)(2,1)}), bf16[32,2,1,48,128]{4,3,1,2,0:T(8,128)(2,1)S(1)}, u32[]{:S(2)}, u32[]{:S(2)}) async-start(bf16[32,2,1,48,128]{4,3,1,2,0:T(8,128)(2,1)} %copy.43), calls=%async_computation.3 | async-start | bytes 1572864 | tf_op jit(solution)/shard_map/all_to_all | solution.py:28
where the time goes:
time: 830 us; the launch traced here: 827 us
  waiting for transfers between devices  679 us (82%)
  starting transfers between devices  68.1 us (8%)
  matrix products  33.8 us (4%)
  other arithmetic  25.7 us (3%)
  local copies, waits for them, and re-layouts  19.3 us (2%)
    all_to_all x1, waiting for transfers between devices, on_device(): lax.all_to_all(joined_far, SEQ, split_axis=0, concat_axis=2, tiled=True)  279 us
    all_to_all x1, waiting for transfers between devices, on_device(): lax.all_to_all(joined_set, SEQ, split_axis=0, concat_axis=2, tiled=True)  279 us
    all_to_all x4, waiting for transfers between devices, exchange_in_order(): out = lax.all_to_all(out, axes[k], k, k, tiled=True)  120 us
    all_to_all x1, starting transfers between devices, on_device(): lax.all_to_all(joined_far, SEQ, split_axis=0, concat_axis=2, tiled=True)  34.3 us
    all_to_all x4, starting transfers between devices, exchange_in_order(): out = lax.all_to_all(out, axes[k], k, k, tiled=True)  21.8 us
    dot_general x8, matrix products, one_block(): jnp.dot(shares, values, preferred_element_type=jnp.float32)  20.6 us
  transfers between devices with their start and end apart: 6, of which 4 were waited for; matrix products, arithmetic and copies ran while one was open for 7% of the time, Pallas kernels for 0%

commit v1 on v0

v1 whole, which is shorter than its diff:
```python
import math

import jax
import jax.numpy as jnp
from jax import lax
from jax.experimental import pallas as pl
from jax.experimental.pallas import tpu as pltpu
from jax.sharding import PartitionSpec as P

MESH = pl.DeviceIdType.MESH
TILE = 8
Q_DEVICES = 4
AUDIO_BLOCKS = 3


def softmax_parts(scores, visible, scale):
    scores = jnp.where(visible, scores * scale, -1e30)
    row_max = jnp.max(scores, axis=1, keepdims=True)
    weights = jnp.exp(scores - row_max)
    return weights.astype(jnp.bfloat16), jnp.sum(weights, axis=1, keepdims=True)


def attend(queries, key_rows, values, visible, scale):
    scores = lax.dot_general(
        queries, key_rows, (((1,), (1,)), ((), ())), preferred_element_type=jnp.float32
    )
    weights, total = softmax_parts(scores, visible, scale)
    return jnp.dot(weights, values, preferred_element_type=jnp.float32) / total


def audio_tokens(count, rows):
    extra = rows - TILE
    column = lax.broadcasted_iota(jnp.int32, (1, count * rows), 1)
    rest = column - count * TILE
    device_first = lax.div(column, TILE)
    device_rest = lax.div(rest, extra)
    first = device_first * rows + (column - device_first * TILE)
    last = device_rest * rows + TILE + (rest - device_rest * extra)
    return jnp.where(rest >= 0, last, first)


def half_rows(tiles):
    return lax.broadcasted_iota(jnp.int32, tiles.shape, 1) < TILE // 2


def swap_halves(tiles):
    return jnp.concatenate([tiles[:, TILE // 2 :], tiles[:, : TILE // 2]], axis=1)


def exchange_and_attend(
    lens,
    gates,
    video_self,
    video_far,
    audio,
    video_out,
    audio_out,
    got_self,
    got_far,
    got_audio,
    audio_sets,
    made_video,
    made_audio,
    mixed_audio,
    sent,
    arrived,
    out_sent,
    out_arrived,
):
    me = lax.axis_index("seq")
    count = got_self.shape[1]
    chips = count // 2
    head_size = got_self.shape[3]
    video_rows = got_self.shape[2]
    audio_rows = got_audio.shape[1] // 6
    scale = 1.0 / math.sqrt(head_size)

    def partner(i):
        step = lax.div(i, 2)
        distance = chips // 2 - lax.div(step + 1, 2)
        offset = distance * (1 - 2 * lax.rem(step, 2)) + chips
        chip = lax.rem(lax.div(me, 2) + offset, chips)
        return chip * 2 + lax.rem(lax.rem(me, 2) + lax.rem(i, 2), 2)

    barrier = pltpu.get_barrier_semaphore()

    def greet(i, carry):
        pl.semaphore_signal(
            barrier, inc=1, device_id={"seq": lax.rem(me + i, count)}, device_id_type=MESH
        )
        return carry

    lax.fori_loop(1, count, greet, 0)
    pl.semaphore_wait(barrier, count - 1)

    key_values = pl.ds(1, 2)
    moves = (
        (video_self, lambda device: got_self.at[:, device]),
        (video_far.at[:, 0], lambda device: got_far.at[0, device]),
        (audio, lambda device: got_audio.at[device]),
        (video_far.at[:, key_values], lambda device: got_far.at[key_values, device]),
    )

    for j, (source, place) in enumerate(moves):
        pltpu.make_async_copy(source.at[me], place(me), arrived.at[j]).start()
    for j, (source, place) in enumerate(moves):

        def send(i, carry, j=j, source=source, place=place):
            other = partner(i)

            @pl.when(other != me)
            def _():
                pltpu.make_async_remote_copy(
                    src_ref=source.at[other],
                    dst_ref=place(me),
                    send_sem=sent.at[j],
                    recv_sem=arrived.at[j],
                    device_id={"seq": other},
                    device_id_type=MESH,
                ).start()

            return carry

        lax.fori_loop(0, count, send, 0)

    pltpu.make_async_copy(got_audio, got_audio, arrived.at[2]).wait()

    first_rows = count * TILE
    for j in range(6):
        whole = got_audio[:, pl.ds(TILE * j, TILE), :]
        audio_sets[j, pl.ds(0, first_rows)] = whole.reshape(first_rows, head_size)
        tiles = got_audio[:, pl.ds(TILE * (6 + j % 3), TILE), :].astype(jnp.float32)
        tiles = tiles.reshape(count // 2, 2, TILE, head_size)
        even, odd = tiles[:, 0], tiles[:, 1]
        if j < 3:
            odd = swap_halves(odd)
        else:
            even = swap_halves(even)
        joined = jnp.where(half_rows(even), even, odd).astype(jnp.bfloat16)
        audio_sets[j, pl.ds(first_rows, count * TILE // 2)] = joined.reshape(
            count * TILE // 2, head_size
        )

    video_visible = (
        lax.broadcasted_iota(jnp.int32, (1, count * video_rows), 1) < lens[0]
    )
    audio_visible = audio_tokens(count, audio_rows) < lens[1]

    def rows_of(ref):
        return ref[...].reshape(-1, head_size)

    pltpu.make_async_copy(got_self, got_self, arrived.at[0]).wait()

    def send_output(made, out, j, other):
        @pl.when(other != me)
        def _():
            pltpu.make_async_remote_copy(
                src_ref=made.at[other],
                dst_ref=out.at[me],
                send_sem=out_sent.at[j],
                recv_sem=out_arrived.at[j],
                device_id={"seq": other},
                device_id_type=MESH,
            ).start()

        @pl.when(other == me)
        def _():
            pltpu.make_async_copy(made.at[me], out.at[me], out_arrived.at[j]).start()

    def video_block(b, carry):
        first = lax.rem(lax.div(me, Q_DEVICES) + 1 + b, count // Q_DEVICES) * Q_DEVICES
        here = pl.ds(first, Q_DEVICES)
        own = attend(
            rows_of(got_self.at[0, here]),
            rows_of(got_self.at[1]),
            rows_of(got_self.at[2]),
            video_visible,
            scale,
        )
        far = attend(
            rows_of(video_cross_q.at[here]), audio_sets[4], audio_sets[5], audio_visible, scale
        )
        mixed = gates[0:1] * own + gates[1:2] * far
        made_video[here] = mixed.astype(jnp.bfloat16).reshape(Q_DEVICES, video_rows, head_size)

        def send(k, carry):
            send_output(made_video, video_out, 0, first + k)
            return carry

        lax.fori_loop(0, Q_DEVICES, send, 0)
        return carry

    video_cross_q = got_far.at[0]
    pltpu.make_async_copy(video_cross_q, video_cross_q, arrived.at[1]).wait()
    lax.fori_loop(0, count // Q_DEVICES, video_block, 0)

    video_cross_kv = got_far.at[key_values]
    pltpu.make_async_copy(video_cross_kv, video_cross_kv, arrived.at[3]).wait()
    block_rows = count * audio_rows // AUDIO_BLOCKS

    def audio_block(b, carry):
        here = pl.ds(pl.multiple_of(b * block_rows, TILE), block_rows)
        own = attend(audio_sets[0, here], audio_sets[1], audio_sets[2], audio_visible, scale)
        far = attend(
            audio_sets[3, here],
            rows_of(got_far.at[1]),
            rows_of(got_far.at[2]),
            video_visible,
            scale,
        )
        mixed_audio[here] = gates[2:3] * own + gates[3:4] * far
        return carry

    lax.fori_loop(0, AUDIO_BLOCKS, audio_block, 0)

    made_audio[:, pl.ds(0, TILE)] = (
        mixed_audio[pl.ds(0, first_rows)].astype(jnp.bfloat16).reshape(count, TILE, head_size)
    )
    rest = mixed_audio[pl.ds(first_rows, first_rows // 2)].reshape(count // 2, TILE, head_size)
    both = jnp.stack([rest, swap_halves(rest)], axis=1)
    made_audio[:, pl.ds(TILE, TILE)] = both.astype(jnp.bfloat16).reshape(count, TILE, head_size)

    def send_audio(i, carry):
        send_output(made_audio, audio_out, 1, partner(i))
        return carry

    lax.fori_loop(0, count, send_audio, 0)

    others = pl.ds(0, count - 1)
    for j, (source, _) in enumerate(moves):
        gone = source.at[others]
        pltpu.make_async_copy(gone, gone, sent.at[j]).wait()
    for j, (made, out) in enumerate(((made_video, video_out), (made_audio, audio_out))):
        pltpu.make_async_copy(made.at[others], made.at[others], out_sent.at[j]).wait()
        pltpu.make_async_copy(out, out, out_arrived.at[j]).wait()


def on_device(video_qkv, video_cross, audio_qkv, audio_cross, lengths, timestep, gate_table):
    count = lax.axis_size("seq")
    clip_count, head_count = video_qkv.shape[:2]
    video_rows, head_size = video_qkv.shape[3:]
    audio_rows = audio_qkv.shape[3]
    if clip_count * head_count != count or audio_rows != TILE * 3 // 2:
        raise ValueError("unexpected shapes")
    me = lax.axis_index("seq")
    clip, head = lax.div(me, head_count), lax.rem(me, head_count)

    lens = lax.dynamic_slice(lengths, (0, clip), (2, 1)).reshape(2)
    gates = lax.dynamic_slice(
        gate_table, (timestep[0], 0, head, 0), (1, gate_table.shape[1], 1, head_size)
    ).reshape(gate_table.shape[1], head_size)

    def pairs(tensor):
        return tensor.reshape((count,) + tensor.shape[2:])

    audio = jnp.concatenate([pairs(audio_qkv), pairs(audio_cross)], axis=1)
    tile_rows = audio[:, :, :TILE].reshape(count, 6 * TILE, head_size)
    rest = audio[:, :, TILE:].reshape(count, 2, 3, TILE // 2, head_size)
    rest = jnp.swapaxes(rest, 1, 2).reshape(count, 3 * TILE, head_size)
    audio = jnp.concatenate([tile_rows, rest], axis=1)

    bf16 = jnp.bfloat16
    video_out, audio_out = pl.pallas_call(
        exchange_and_attend,
        out_shape=(
            jax.ShapeDtypeStruct((count, video_rows, head_size), bf16),
            jax.ShapeDtypeStruct((count, 2 * TILE, head_size), bf16),
        ),
        in_specs=[
            pl.BlockSpec(memory_space=pltpu.SMEM),
            pl.BlockSpec(memory_space=pltpu.VMEM),
            pl.BlockSpec(memory_space=pl.ANY),
            pl.BlockSpec(memory_space=pl.ANY),
            pl.BlockSpec(memory_space=pl.ANY),
        ],
        out_specs=[pl.BlockSpec(memory_space=pl.ANY)] * 2,
        scratch_shapes=[
            pltpu.VMEM((3, count, video_rows, head_size), bf16),
            pltpu.VMEM((3, count, video_rows, head_size), bf16),
            pltpu.VMEM((count, 6 * audio_rows, head_size), bf16),
            pltpu.VMEM((6, count * audio_rows, head_size), bf16),
            pltpu.VMEM((count, video_rows, head_size), bf16),
            pltpu.VMEM((count, 2 * TILE, head_size), bf16),
            pltpu.VMEM((count * audio_rows, head_size), jnp.float32),
            pltpu.SemaphoreType.DMA((4,)),
            pltpu.SemaphoreType.DMA((4,)),
            pltpu.SemaphoreType.DMA((2,)),
            pltpu.SemaphoreType.DMA((2,)),
        ],
        compiler_params=pltpu.CompilerParams(
            collective_id=0, has_side_effects=True, vmem_limit_bytes=60 * 2**20
        ),
    )(lens, gates, pairs(video_qkv), pairs(video_cross), audio)
    return (
        video_out.reshape(clip_count, head_count, video_rows, head_size),
        audio_out[:, :audio_rows].reshape(clip_count, head_count, audio_rows, head_size),
    )


def solution(mesh):
    tokens = P("groups", None, None, "seq", None)
    made = P("groups", None, "seq", None)
    return jax.shard_map(
        on_device,
        mesh=mesh,
        in_specs=(tokens, tokens, tokens, tokens, P(None, "groups"), P("groups"), P()),
        out_specs=(made, made),
        check_vma=False,
    )
```

time: 830 us -> 643 us (0.77)
  waiting for transfers between devices: 679 us -> 0 us
  Pallas kernels: 0 us -> 632 us
  starting transfers between devices: 68.1 us -> 0 us
  matrix products: 33.8 us -> 0 us
  other arithmetic: 25.7 us -> 1.21 us
  local copies, waits for them, and re-layouts: 19.3 us -> 7.9 us
    all_to_all x6 -> x0, waiting for transfers between devices: 679 us -> none  [the longest x1 279 us: on_device(): lax.all_to_all(joined_far, SEQ, split_axis=0, concat_axis=2, tiled=True)]
    pallas_call x0 -> x1, Pallas kernels: none -> 632 us  [on_device(): pl.pallas_call(exchange_and_attend, out_shape=(jax.ShapeDtypeStruct((coun...]
    all_to_all x6 -> x0, starting transfers between devices: 68.1 us -> none  [the longest x1 34.3 us: on_device(): lax.all_to_all(joined_far, SEQ, split_axis=0, concat_axis=2, tiled=True)]
    dot_general x16 -> x0, matrix products: 33.8 us -> none  [the longest x8 20.6 us: one_block(): jnp.dot(shares, values, preferred_element_type=jnp.float32)]
    reduce_sum x11 -> x0, other arithmetic: 15.3 us -> none  [the longest x8 12.9 us: one_block(): row_total = jnp.sum(weights, axis=1, keepdims=True)]
  transfers between devices with their start and end apart: 6 -> 0, of which waited for: 4 -> 0; matrix products, arithmetic and copies ran while one was open for 7% -> 0% of each run, Pallas kernels for 0% -> 0%
where the time goes in v1:
time: 643 us
  Pallas kernels  632 us (98%)
  local copies, waits for them, and re-layouts  7.9 us (1%)
    pallas_call x1, Pallas kernels, on_device(): pl.pallas_call(exchange_and_attend, out_shape=(jax.ShapeDtypeStruct((coun...  632 us

profile of v1, /device:TPU:37, one launch (start us, length us, event | category | flops | bytes accessed | tf_op | source)
XLA Modules:
  0.0 642.8 jit_solution(15373063040841202301)
XLA Ops:
  0.6 0.0 copy-start
  0.6 0.0 copy-start.1
  1.5 1.4 dynamic-slice_reduce_fusion.lens
  2.8 0.0 copy-done
  2.8 0.6 constant_dynamic-slice_fusion
  3.4 1.2 copy.10
  4.6 0.0 copy-done.1
  4.7 0.2 copy.11
  4.9 0.1 fusion
  4.9 0.5 copy.16
  5.5 0.3 copy.13
  5.8 1.1 pad_maximum_fusion.audio
  6.9 632.1 %shard_map.86 = (bf16[64,48,128]{2,1,0:T(8,128)(2,1)}, bf16[64,16,128]{2,1,0:T(8,128)(2,1)}) custom-call(s32[2]{0:T(128)} %dynamic-slice_reduce_fusion.lens, f32[4,128]{1,0:T(4,128)} %bitcast.30, bf16[64,3,48,128]{3,2,1,0:T(8,128)(2,1)} %bitcast.24, bf16[64,3,48,128]{3,2,1,0:T(8,128)(2,1)} %bitcast.25, bf16[64,72,128]{2,1,0:T(8,128)(2,1)} %pad_maximum_fusion.audio), custom_call_target="tpu_custom_call" | custom-call | tf_op jit(solution)/shard_map/pallas_call | solution.py:263
  639.0 1.7 copy.14
  640.7 2.1 copy.19
  (1 shorter events, 0.0 us)
Async XLA Ops:
  0.6 2.2 copy-start
  0.6 4.0 copy-start.1

commit v2 on v1

v2 whole, which is shorter than its diff:
```python
import functools
import math

import jax
import jax.numpy as jnp
from jax import lax
from jax.experimental import pallas as pl
from jax.experimental.pallas import tpu as pltpu
from jax.sharding import PartitionSpec as P

MESH = pl.DeviceIdType.MESH
HALF_TILE = 4
Q_DEVICES = 4
AUDIO_BLOCKS = 3


def dot_rows(left, right):
    return lax.dot_general(
        left, right, (((1,), (1,)), ((), ())), preferred_element_type=jnp.float32
    )


def attend(queries, key_rows, values, visible, scale):
    scores = jnp.where(visible, dot_rows(queries, key_rows) * scale, -1e30)
    row_max = jnp.max(scores, axis=1, keepdims=True)
    weights = jnp.exp(scores - row_max)
    row_total = jnp.sum(weights, axis=1, keepdims=True)
    found = jnp.dot(weights.astype(jnp.bfloat16), values, preferred_element_type=jnp.float32)
    return found / row_total


def attend_part(queries, key_rows, values, visible, scale):
    scores = jnp.where(visible, dot_rows(key_rows, queries) * scale, -1e30)
    top = jnp.max(scores, axis=0, keepdims=True)
    weights = jnp.exp(scores - top)
    total = jnp.sum(weights, axis=0, keepdims=True)
    found = lax.dot_general(
        values,
        weights.astype(jnp.bfloat16),
        (((0,), (0,)), ((), ())),
        preferred_element_type=jnp.float32,
    )
    return found, top, total


def exchange_and_attend(
    head_count,
    lengths,
    timestep,
    gate_table,
    video_self,
    video_far,
    video_far_halves,
    audio_self_raw,
    audio_far_raw,
    video_out,
    audio_out,
    gates,
    raw,
    audio,
    got_self,
    got_query,
    got_kv,
    got_audio,
    got_audio_query,
    audio_sets,
    part_video,
    made_video,
    part_audio,
    half_found,
    half_stats,
    got_stats,
    made_audio,
    loaded,
    sent,
    arrived,
    stats_sent,
    stats_arrived,
    out_sent,
    out_arrived,
):
    me = lax.axis_index("seq")
    count = got_self.shape[1]
    half = count // 2
    chips = count // 2
    head_size = got_self.shape[3]
    video_rows = got_self.shape[2]
    audio_rows = raw.shape[3]
    audio_total = count * audio_rows
    scale = 1.0 / math.sqrt(head_size)
    my_chip, my_core = lax.div(me, 2), lax.rem(me, 2)
    mirror = lax.rem(me + half, count)
    my_half, my_place = lax.div(me, half), lax.rem(me, half)

    def at_offset(offset, core):
        return lax.rem(my_chip + offset + chips, chips) * 2 + core

    def partner(i):
        step = lax.div(i, 2)
        offset = (chips // 2 - lax.div(step + 1, 2)) * (1 - 2 * lax.rem(step, 2))
        return at_offset(offset, lax.rem(my_core + lax.rem(i, 2), 2))

    def near_target(i):
        step, core = lax.div(i, 2), lax.rem(i, 2)
        offset = (chips // 4 - lax.div(step + 1, 2)) * (1 - 2 * lax.rem(step, 2)) * (1 - 2 * core)
        slot = (chips // 4 - core - offset) * 2 + my_core
        return at_offset(offset, core), slot

    barrier = pltpu.get_barrier_semaphore()

    def greet(i, carry):
        pl.semaphore_signal(
            barrier, inc=1, device_id={"seq": lax.rem(me + i, count)}, device_id_type=MESH
        )
        return carry

    lax.fori_loop(1, count, greet, 0)

    loads = (
        pltpu.make_async_copy(audio_self_raw, raw.at[0], loaded.at[0]),
        pltpu.make_async_copy(audio_far_raw, raw.at[1], loaded.at[1]),
        pltpu.make_async_copy(gate_table, gates, loaded.at[2]),
    )
    for load in loads:
        load.start()
    for load in loads:
        load.wait()
    for side in range(2):
        for clip in range(raw.shape[1]):
            rows = raw[side, clip].astype(jnp.float32)
            rows = rows.reshape(3 * audio_rows, head_count, head_size)
            rows = jnp.swapaxes(rows, 0, 1).astype(jnp.bfloat16)
            audio[pl.ds(clip * head_count, head_count), pl.ds(3 * side, 3)] = rows.reshape(
                head_count, 3, audio_rows // HALF_TILE, HALF_TILE, head_size
            )

    pl.semaphore_wait(barrier, count - 1)

    keys_values = pl.ds(1, 2)

    def copy_to(source, place, j, other):
        return pltpu.make_async_remote_copy(
            src_ref=source,
            dst_ref=place,
            send_sem=sent.at[j],
            recv_sem=arrived.at[j],
            device_id={"seq": other},
            device_id_type=MESH,
        )

    def send_kv(i, carry):
        other, slot = near_target(i)
        source = video_far_halves.at[:, lax.rem(other, half), keys_values]
        place = got_kv.at[:, :, slot]

        @pl.when(other != me)
        def _():
            copy_to(source, place, 0, other).start()

        @pl.when(other == me)
        def _():
            pltpu.make_async_copy(source, place, arrived.at[0]).start()

        return carry

    lax.fori_loop(0, half, send_kv, 0)

    def mirror_of(device):
        return lax.rem(device + half, count)

    spread = {
        1: (lambda other: audio.at[other], got_audio.at[me]),
        2: (lambda other: audio.at[mirror_of(other), 3], got_audio_query.at[me]),
        3: (lambda other: video_self.at[other], got_self.at[:, me]),
        4: (lambda other: video_far.at[other, 0], got_query.at[me]),
    }

    def send_all(*kinds):
        for j in kinds:
            pltpu.make_async_copy(spread[j][0](me), spread[j][1], arrived.at[j]).start()

        for j in kinds:

            def send(i, carry, j=j):
                other = partner(i)

                @pl.when(other != me)
                def _():
                    copy_to(spread[j][0](other), spread[j][1], j, other).start()

                return carry

            lax.fori_loop(0, count, send, 0)

    send_all(1)
    send_all(2)
    send_all(3)

    def wait_whole(ref, sem):
        pltpu.make_async_copy(ref, ref, sem).wait()

    step_gates = timestep[0]

    def gate(row, device):
        head = lax.rem(device, head_count)
        return gates[pl.ds(step_gates, 1), row, pl.ds(head, 1), :].reshape(1, head_size)

    wait_whole(got_audio, arrived.at[1])
    wait_whole(got_audio_query, arrived.at[2])
    for j in range(6):
        audio_sets[j] = got_audio[:, j].reshape(audio_total, head_size)
    audio_sets[6] = got_audio_query[...].reshape(audio_total, head_size)
    wait_whole(got_kv, arrived.at[0])

    block = audio_total // AUDIO_BLOCKS
    first_near = lax.rem(my_chip - chips // 4 + my_core + chips, chips) * 2 * video_rows
    position = first_near + lax.broadcasted_iota(jnp.int32, (half * video_rows, block), 0)
    position = jnp.where(
        position >= count * video_rows, position - count * video_rows, position
    )

    def rows_of(ref):
        return ref[...].reshape(-1, head_size)

    def cross_part(i, carry):
        kind, b = lax.div(i, AUDIO_BLOCKS), lax.rem(i, AUDIO_BLOCKS)
        pair = lax.rem(me + kind * half, count)
        side = lax.div(pair, half)
        found, top, total = attend_part(
            audio_sets[3 + 3 * kind, pl.ds(pl.multiple_of(b * block, block), block)],
            rows_of(got_kv.at[side, 0]),
            rows_of(got_kv.at[side, 1]),
            position < lengths[0, lax.div(pair, head_count)],
            scale,
        )
        half_found[i] = found
        half_stats[i] = jnp.concatenate([top, total], axis=0)
        return carry

    lax.fori_loop(0, 2 * AUDIO_BLOCKS, cross_part, 0)
    stats_copy = pltpu.make_async_remote_copy(
        src_ref=half_stats,
        dst_ref=got_stats,
        send_sem=stats_sent,
        recv_sem=stats_arrived,
        device_id={"seq": mirror},
        device_id_type=MESH,
    )
    stats_copy.start()
    send_all(4)

    my_clip = lax.div(me, head_count)
    audio_visible = (
        lax.broadcasted_iota(jnp.int32, (1, audio_total), 1) < lengths[1, my_clip]
    )
    video_visible = (
        lax.broadcasted_iota(jnp.int32, (1, count * video_rows), 1) < lengths[0, my_clip]
    )

    def audio_block(b, carry):
        here = pl.ds(pl.multiple_of(b * block, block), block)
        own = attend(audio_sets[0, here], audio_sets[1], audio_sets[2], audio_visible, scale)
        part_audio[0, here] = gate(2, me) * own
        part_audio[1, here] = jnp.zeros_like(own)
        return carry

    lax.fori_loop(0, AUDIO_BLOCKS, audio_block, 0)

    stats_copy.wait()

    def join_parts(i, carry):
        kind, b = lax.div(i, AUDIO_BLOCKS), lax.rem(i, AUDIO_BLOCKS)
        pair = lax.rem(me + kind * half, count)
        mine = half_stats[i]
        theirs = got_stats[(1 - kind) * AUDIO_BLOCKS + b]
        top = jnp.maximum(mine[0:1], theirs[0:1])
        weight = jnp.exp(mine[0:1] - top)
        total = mine[1:2] * weight + theirs[1:2] * jnp.exp(theirs[0:1] - top)
        found = half_found[i] * (weight / total)
        here = pl.ds(pl.multiple_of(b * block, block), block)
        part_audio[kind, here] = part_audio[kind, here] + gate(3, pair) * found.T
        return carry

    lax.fori_loop(0, 2 * AUDIO_BLOCKS, join_parts, 0)
    for kind in range(2):
        side = lax.rem(my_half + kind, 2)
        made_audio[side] = (
            part_audio[kind]
            .astype(jnp.bfloat16)
            .reshape(count, audio_rows // HALF_TILE, HALF_TILE, head_size)
        )

    def send_output(made, place, j, other):
        @pl.when(other != me)
        def _():
            pltpu.make_async_remote_copy(
                src_ref=made,
                dst_ref=place,
                send_sem=out_sent.at[j],
                recv_sem=out_arrived.at[j],
                device_id={"seq": other},
                device_id_type=MESH,
            ).start()

        @pl.when(other == me)
        def _():
            pltpu.make_async_copy(made, place, out_arrived.at[j]).start()

    def video_self_block(b, carry):
        here = pl.ds(b * Q_DEVICES, Q_DEVICES)
        own = attend(
            rows_of(got_self.at[0, here]),
            rows_of(got_self.at[1]),
            rows_of(got_self.at[2]),
            video_visible,
            scale,
        )
        part_video[here] = (gate(0, me) * own).reshape(Q_DEVICES, video_rows, head_size)
        return carry

    def send_audio(i, carry):
        other = partner(i)
        send_output(made_audio.at[:, other], audio_out.at[my_half, :, my_place], 1, other)
        return carry

    lax.fori_loop(0, count, send_audio, 0)

    wait_whole(got_self, arrived.at[3])
    lax.fori_loop(0, count // Q_DEVICES, video_self_block, 0)

    wait_whole(got_query, arrived.at[4])

    def video_cross_block(b, carry):
        first = lax.rem(lax.div(me, Q_DEVICES) + 1 + b, count // Q_DEVICES) * Q_DEVICES
        here = pl.ds(first, Q_DEVICES)
        far = attend(
            rows_of(got_query.at[here]), audio_sets[4], audio_sets[5], audio_visible, scale
        )
        mixed = part_video[here] + (gate(1, me) * far).reshape(Q_DEVICES, video_rows, head_size)
        made_video[here] = mixed.astype(jnp.bfloat16)

        def send(k, carry):
            other = first + k
            send_output(made_video.at[other], video_out.at[me], 0, other)
            return carry

        lax.fori_loop(0, Q_DEVICES, send, 0)
        return carry

    lax.fori_loop(0, count // Q_DEVICES, video_cross_block, 0)

    others = pl.ds(0, count - 1)
    wait_whole(video_far_halves.at[:, pl.ds(0, half - 1), keys_values], sent.at[0])
    wait_whole(audio.at[others], sent.at[1])
    wait_whole(audio.at[others, 3], sent.at[2])
    wait_whole(video_self.at[others], sent.at[3])
    wait_whole(video_far.at[others, 0], sent.at[4])
    wait_whole(made_video.at[others], out_sent.at[0])
    wait_whole(made_audio.at[:, others], out_sent.at[1])
    wait_whole(video_out, out_arrived.at[0])
    wait_whole(audio_out, out_arrived.at[1])


def on_device(video_qkv, video_cross, audio_qkv, audio_cross, lengths, timestep, gate_table):
    count = lax.axis_size("seq")
    half = count // 2
    clip_count, head_count = video_qkv.shape[:2]
    video_rows, head_size = video_qkv.shape[3:]
    audio_rows = audio_qkv.shape[3]
    if clip_count * head_count != count or audio_rows % HALF_TILE:
        raise ValueError("unexpected shapes")
    quarters = audio_rows // HALF_TILE
    audio_total = count * audio_rows
    block = audio_total // AUDIO_BLOCKS

    video_self = video_qkv.reshape(count, 3, video_rows, head_size)
    video_far = video_cross.reshape(count, 3, video_rows, head_size)
    video_far_halves = video_cross.reshape(2, half, 3, video_rows, head_size)

    def heads_inside(tensor):
        return jnp.transpose(tensor, (0, 2, 3, 1, 4))

    bf16, f32 = jnp.bfloat16, jnp.float32
    anywhere = pl.BlockSpec(memory_space=pl.ANY)
    scalars = pl.BlockSpec(memory_space=pltpu.SMEM)
    video_out, audio_out = pl.pallas_call(
        functools.partial(exchange_and_attend, head_count),
        out_shape=(
            jax.ShapeDtypeStruct((count, video_rows, head_size), bf16),
            jax.ShapeDtypeStruct((2, 2, half, quarters, HALF_TILE, head_size), bf16),
        ),
        in_specs=[scalars, scalars] + [anywhere] * 6,
        out_specs=[anywhere] * 2,
        scratch_shapes=[
            pltpu.VMEM(gate_table.shape, f32),
            pltpu.VMEM((2, clip_count, 3, audio_rows, head_count, head_size), bf16),
            pltpu.VMEM((count, 6, quarters, HALF_TILE, head_size), bf16),
            pltpu.VMEM((3, count, video_rows, head_size), bf16),
            pltpu.VMEM((count, video_rows, head_size), bf16),
            pltpu.VMEM((2, 2, half, video_rows, head_size), bf16),
            pltpu.VMEM((count, 6, quarters, HALF_TILE, head_size), bf16),
            pltpu.VMEM((count, quarters, HALF_TILE, head_size), bf16),
            pltpu.VMEM((7, audio_total, head_size), bf16),
            pltpu.VMEM((count, video_rows, head_size), f32),
            pltpu.VMEM((count, video_rows, head_size), bf16),
            pltpu.VMEM((2, audio_total, head_size), f32),
            pltpu.VMEM((2 * AUDIO_BLOCKS, head_size, block), f32),
            pltpu.VMEM((2 * AUDIO_BLOCKS, 2, block), f32),
            pltpu.VMEM((2 * AUDIO_BLOCKS, 2, block), f32),
            pltpu.VMEM((2, count, quarters, HALF_TILE, head_size), bf16),
            pltpu.SemaphoreType.DMA((3,)),
            pltpu.SemaphoreType.DMA((5,)),
            pltpu.SemaphoreType.DMA((5,)),
            pltpu.SemaphoreType.DMA,
            pltpu.SemaphoreType.DMA,
            pltpu.SemaphoreType.DMA((2,)),
            pltpu.SemaphoreType.DMA((2,)),
        ],
        compiler_params=pltpu.CompilerParams(
            collective_id=0, has_side_effects=True, vmem_limit_bytes=62 * 2**20
        ),
    )(
        lengths,
        timestep,
        gate_table,
        video_self,
        video_far,
        video_far_halves,
        heads_inside(audio_qkv),
        heads_inside(audio_cross),
    )
    audio_sum = audio_out[0].astype(f32) + audio_out[1].astype(f32)
    return (
        video_out.reshape(clip_count, head_count, video_rows, head_size),
        audio_sum.astype(bf16).reshape(clip_count, head_count, audio_rows, head_size),
    )


def solution(mesh):
    tokens = P("groups", None, None, "seq", None)
    made = P("groups", None, "seq", None)
    return jax.shard_map(
        on_device,
        mesh=mesh,
        in_specs=(tokens, tokens, tokens, tokens, P(None, "groups"), P("groups"), P()),
        out_specs=(made, made),
        check_vma=False,
    )
```

time: 643 us -> 600 us (0.933)
  Pallas kernels: 632 us -> 594 us
    pallas_call x1, Pallas kernels: 632 us -> 594 us  [on_device(): pl.pallas_call(functools.partial(exchange_and_attend, head_count), out_sh...]
where the time goes in v2:
time: 600 us; the launch traced here: 599 us
  Pallas kernels  594 us (99%)
    pallas_call x1, Pallas kernels, on_device(): pl.pallas_call(functools.partial(exchange_and_attend, head_count), out_sh...  594 us

profile of v2, /device:TPU:37, one launch (start us, length us, event | category | flops | bytes accessed | tf_op | source)
XLA Modules:
  0.0 599.3 jit_solution(13187229311693866826)
XLA Ops:
  1.3 594.1 %shard_map.86 = (bf16[64,48,128]{2,1,0:T(8,128)(2,1)}, bf16[2,2,32,3,4,128]{5,4,3,2,1,0:T(4,128)(2,1)}) custom-call(s32[2,4]{1,0:T(2,128)} %lengths.1, s32[1]{0:T(128)S(6)} %copy.15.timestep, f32[50,4,16,128]{3,2,1,0:T(8,128)} %gate_table.1, bf16[64,3,48,128]{3,2,1,0:T(8,128)(2,1)} %bitcast.9, bf16[64,3,48,128]{3,2,1,0:T(8,128)(2,1)} %bitcast.7, ...), custom_call_target="tpu_custom_call" | custom-call | tf_op jit(solution)/shard_map/pallas_call | solution.py:386
  595.4 1.1 add_convert_fusion
  596.6 0.7 copy.13
  597.3 2.1 copy.16
  (1 shorter events, 0.0 us)

commit v3 on v2

--- a/solution.py
+++ b/solution.py
@@ -71,6 +71,10 @@
     half_stats,
     got_stats,
     made_audio,
+    got_made_audio,
+    final_audio,
+    known_quarter,
+    known_half,
     loaded,
     sent,
     arrived,
@@ -106,16 +110,6 @@
         slot = (chips // 4 - core - offset) * 2 + my_core
         return at_offset(offset, core), slot
 
-    barrier = pltpu.get_barrier_semaphore()
-
-    def greet(i, carry):
-        pl.semaphore_signal(
-            barrier, inc=1, device_id={"seq": lax.rem(me + i, count)}, device_id_type=MESH
-        )
-        return carry
-
-    lax.fori_loop(1, count, greet, 0)
-
     loads = (
         pltpu.make_async_copy(audio_self_raw, raw.at[0], loaded.at[0]),
         pltpu.make_async_copy(audio_far_raw, raw.at[1], loaded.at[1]),
@@ -123,6 +117,63 @@
     )
     for load in loads:
         load.start()
+
+    reach = chips // 8
+    barrier = pltpu.get_barrier_semaphore()
+
+    def greet(i, carry):
+        other = at_offset(lax.div(i, 2) - reach, lax.rem(i, 2))
+
+        @pl.when(other != me)
+        def _():
+            pl.semaphore_signal(barrier, inc=1, device_id={"seq": other}, device_id_type=MESH)
+
+        return carry
+
+    lax.fori_loop(0, 4 * reach + 2, greet, 0)
+    pl.semaphore_wait(barrier, 4 * reach + 1)
+
+    def pass_on(known, distance):
+        for offset in (-distance, distance):
+            pl.semaphore_signal(
+                known,
+                inc=1,
+                device_id={"seq": at_offset(offset, my_core)},
+                device_id_type=MESH,
+            )
+
+    pass_on(known_quarter, reach)
+
+    keys_values = pl.ds(1, 2)
+
+    def copy_to(source, place, j, other):
+        return pltpu.make_async_remote_copy(
+            src_ref=source,
+            dst_ref=place,
+            send_sem=sent.at[j],
+            recv_sem=arrived.at[j],
+            device_id={"seq": other},
+            device_id_type=MESH,
+        )
+
+    def send_kv(i, carry):
+        other, slot = near_target(i)
+        source = video_far_halves.at[:, lax.rem(other, half), keys_values]
+        place = got_kv.at[:, :, slot]
+
+        @pl.when(other != me)
+        def _():
+            copy_to(source, place, 0, other).start()
+
+        @pl.when(other == me)
+        def _():
+            pltpu.make_async_copy(source, place, arrived.at[0]).start()
+
+        return carry
+
+    first_close = 4 * (chips // 4 - reach) - 2
+    lax.fori_loop(first_close, half, send_kv, 0)
+
     for load in loads:
         load.wait()
     for side in range(2):
@@ -134,36 +185,10 @@
                 head_count, 3, audio_rows // HALF_TILE, HALF_TILE, head_size
             )
 
-    pl.semaphore_wait(barrier, count - 1)
-
-    keys_values = pl.ds(1, 2)
-
-    def copy_to(source, place, j, other):
-        return pltpu.make_async_remote_copy(
-            src_ref=source,
-            dst_ref=place,
-            send_sem=sent.at[j],
-            recv_sem=arrived.at[j],
-            device_id={"seq": other},
-            device_id_type=MESH,
-        )
-
-    def send_kv(i, carry):
-        other, slot = near_target(i)
-        source = video_far_halves.at[:, lax.rem(other, half), keys_values]
-        place = got_kv.at[:, :, slot]
-
-        @pl.when(other != me)
-        def _():
-            copy_to(source, place, 0, other).start()
-
-        @pl.when(other == me)
-        def _():
-            pltpu.make_async_copy(source, place, arrived.at[0]).start()
-
-        return carry
-
-    lax.fori_loop(0, half, send_kv, 0)
+    pl.semaphore_wait(known_quarter, 2)
+    pass_on(known_half, 2 * reach)
+    lax.fori_loop(0, first_close, send_kv, 0)
+    pl.semaphore_wait(known_half, 2)
 
     def mirror_of(device):
         return lax.rem(device + half, count)
@@ -320,7 +345,7 @@
 
     def send_audio(i, carry):
         other = partner(i)
-        send_output(made_audio.at[:, other], audio_out.at[my_half, :, my_place], 1, other)
+        send_output(made_audio.at[:, other], got_made_audio.at[my_half, :, my_place], 1, other)
         return carry
 
     lax.fori_loop(0, count, send_audio, 0)
@@ -331,7 +356,9 @@
     wait_whole(got_query, arrived.at[4])
 
     def video_cross_block(b, carry):
-        first = lax.rem(lax.div(me, Q_DEVICES) + 1 + b, count // Q_DEVICES) * Q_DEVICES
+        blocks = count // Q_DEVICES
+        offset = (blocks // 2 - lax.div(b + 1, 2)) * (1 - 2 * lax.rem(b, 2))
+        first = lax.rem(lax.div(me, Q_DEVICES) + offset + blocks, blocks) * Q_DEVICES
         here = pl.ds(first, Q_DEVICES)
         far = attend(
             rows_of(got_query.at[here]), audio_sets[4], audio_sets[5], audio_visible, scale
@@ -348,6 +375,15 @@
         return carry
 
     lax.fori_loop(0, count // Q_DEVICES, video_cross_block, 0)
+
+    wait_whole(got_made_audio, out_arrived.at[1])
+    whole_audio = got_made_audio[0].astype(jnp.float32) + got_made_audio[1].astype(jnp.float32)
+    whole_audio = whole_audio.reshape(count // head_count, head_count, audio_rows, head_size)
+    for clip in range(count // head_count):
+        final_audio[clip] = jnp.swapaxes(whole_audio[clip], 0, 1).astype(jnp.bfloat16)
+    keep_audio = pltpu.make_async_copy(final_audio, audio_out, loaded.at[0])
+    keep_audio.start()
+    keep_audio.wait()
 
     others = pl.ds(0, count - 1)
     wait_whole(video_far_halves.at[:, pl.ds(0, half - 1), keys_values], sent.at[0])
@@ -358,7 +394,6 @@
     wait_whole(made_video.at[others], out_sent.at[0])
     wait_whole(made_audio.at[:, others], out_sent.at[1])
     wait_whole(video_out, out_arrived.at[0])
-    wait_whole(audio_out, out_arrived.at[1])
 
 
 def on_device(video_qkv, video_cross, audio_qkv, audio_cross, lengths, timestep, gate_table):
@@ -387,7 +422,7 @@
         functools.partial(exchange_and_attend, head_count),
         out_shape=(
             jax.ShapeDtypeStruct((count, video_rows, head_size), bf16),
-            jax.ShapeDtypeStruct((2, 2, half, quarters, HALF_TILE, head_size), bf16),
+            jax.ShapeDtypeStruct((clip_count, audio_rows, head_count, head_size), bf16),
         ),
         in_specs=[scalars, scalars] + [anywhere] * 6,
         out_specs=[anywhere] * 2,
@@ -408,6 +443,10 @@
             pltpu.VMEM((2 * AUDIO_BLOCKS, 2, block), f32),
             pltpu.VMEM((2 * AUDIO_BLOCKS, 2, block), f32),
             pltpu.VMEM((2, count, quarters, HALF_TILE, head_size), bf16),
+            pltpu.VMEM((2, 2, half, quarters, HALF_TILE, head_size), bf16),
+            pltpu.VMEM((clip_count, audio_rows, head_count, head_size), bf16),
+            pltpu.SemaphoreType.REGULAR,
+            pltpu.SemaphoreType.REGULAR,
             pltpu.SemaphoreType.DMA((3,)),
             pltpu.SemaphoreType.DMA((5,)),
             pltpu.SemaphoreType.DMA((5,)),
@@ -429,10 +468,9 @@
         heads_inside(audio_qkv),
         heads_inside(audio_cross),
     )
-    audio_sum = audio_out[0].astype(f32) + audio_out[1].astype(f32)
     return (
         video_out.reshape(clip_count, head_count, video_rows, head_size),
-        audio_sum.astype(bf16).reshape(clip_count, head_count, audio_rows, head_size),
+        jnp.swapaxes(audio_out, 1, 2),
     )
 
 

time: 600 us -> 593 us (0.988)
  Pallas kernels: 594 us -> 588 us
    pallas_call x1, Pallas kernels: 594 us -> 588 us  [on_device(): pl.pallas_call(functools.partial(exchange_and_attend, head_count), out_sh...]
where the time goes in v3:
time: 593 us
  Pallas kernels  588 us (99%)
    pallas_call x1, Pallas kernels, on_device(): pl.pallas_call(functools.partial(exchange_and_attend, head_count), out_sh...  588 us

profile of v3, /device:TPU:37, one launch (start us, length us, event | category | flops | bytes accessed | tf_op | source)
XLA Modules:
  0.0 592.6 jit_solution(8796625399914457960)
XLA Ops:
  1.3 587.6 %shard_map.86 = (bf16[64,48,128]{2,1,0:T(8,128)(2,1)}, bf16[4,12,16,128]{3,2,1,0:T(8,128)(2,1)}) custom-call(s32[2,4]{1,0:T(2,128)} %lengths.1, s32[1]{0:T(128)S(6)} %copy.11.timestep, f32[50,4,16,128]{3,2,1,0:T(8,128)} %gate_table.1, bf16[64,3,48,128]{3,2,1,0:T(8,128)(2,1)} %bitcast.9, bf16[64,3,48,128]{3,2,1,0:T(8,128)(2,1)} %bitcast.7, ...), custom_call_target="tpu_custom_call" | custom-call | tf_op jit(solution)/shard_map/pallas_call | solution.py:421
  588.9 2.1 copy.12
  591.0 1.6 copy.13

commit v4 on v3

--- a/solution.py
+++ b/solution.py
@@ -40,13 +40,13 @@
         (((0,), (0,)), ((), ())),
         preferred_element_type=jnp.float32,
     )
-    return found, top, total
+    return found / total, top + jnp.log(total)
 
 
 def exchange_and_attend(
     head_count,
-    lengths,
     timestep,
+    lengths_given,
     gate_table,
     video_self,
     video_far,
@@ -55,6 +55,7 @@
     audio_far_raw,
     video_out,
     audio_out,
+    lengths,
     gates,
     raw,
     audio,
@@ -73,8 +74,7 @@
     made_audio,
     got_made_audio,
     final_audio,
-    known_quarter,
-    known_half,
+    known,
     loaded,
     sent,
     arrived,
@@ -114,15 +114,15 @@
         pltpu.make_async_copy(audio_self_raw, raw.at[0], loaded.at[0]),
         pltpu.make_async_copy(audio_far_raw, raw.at[1], loaded.at[1]),
         pltpu.make_async_copy(gate_table, gates, loaded.at[2]),
+        pltpu.make_async_copy(lengths_given, lengths, loaded.at[3]),
     )
     for load in loads:
         load.start()
 
-    reach = chips // 8
     barrier = pltpu.get_barrier_semaphore()
 
     def greet(i, carry):
-        other = at_offset(lax.div(i, 2) - reach, lax.rem(i, 2))
+        other = at_offset(lax.div(i, 2) - 1, lax.rem(i, 2))
 
         @pl.when(other != me)
         def _():
@@ -130,19 +130,17 @@
 
         return carry
 
-    lax.fori_loop(0, 4 * reach + 2, greet, 0)
-    pl.semaphore_wait(barrier, 4 * reach + 1)
-
-    def pass_on(known, distance):
+    lax.fori_loop(0, 6, greet, 0)
+    pl.semaphore_wait(barrier, 5)
+
+    def pass_on(step, distance):
         for offset in (-distance, distance):
             pl.semaphore_signal(
-                known,
+                known.at[step],
                 inc=1,
                 device_id={"seq": at_offset(offset, my_core)},
                 device_id_type=MESH,
             )
-
-    pass_on(known_quarter, reach)
 
     keys_values = pl.ds(1, 2)
 
@@ -171,8 +169,15 @@
 
         return carry
 
-    first_close = 4 * (chips // 4 - reach) - 2
-    lax.fori_loop(first_close, half, send_kv, 0)
+    quarter = chips // 4
+    reach, unsent = 1, half
+    for step in range(known.shape[0]):
+        pass_on(step, reach)
+        start = max(0, 4 * (quarter - reach) - 2)
+        lax.fori_loop(start, unsent, send_kv, 0)
+        unsent, reach = start, 2 * reach
+        if step < known.shape[0] - 1:
+            pl.semaphore_wait(known.at[step], 2)
 
     for load in loads:
         load.wait()
@@ -185,10 +190,7 @@
                 head_count, 3, audio_rows // HALF_TILE, HALF_TILE, head_size
             )
 
-    pl.semaphore_wait(known_quarter, 2)
-    pass_on(known_half, 2 * reach)
-    lax.fori_loop(0, first_close, send_kv, 0)
-    pl.semaphore_wait(known_half, 2)
+    pl.semaphore_wait(known.at[known.shape[0] - 1], 2)
 
     def mirror_of(device):
         return lax.rem(device + half, count)
@@ -251,7 +253,7 @@
         kind, b = lax.div(i, AUDIO_BLOCKS), lax.rem(i, AUDIO_BLOCKS)
         pair = lax.rem(me + kind * half, count)
         side = lax.div(pair, half)
-        found, top, total = attend_part(
+        found, level = attend_part(
             audio_sets[3 + 3 * kind, pl.ds(pl.multiple_of(b * block, block), block)],
             rows_of(got_kv.at[side, 0]),
             rows_of(got_kv.at[side, 1]),
@@ -259,7 +261,7 @@
             scale,
         )
         half_found[i] = found
-        half_stats[i] = jnp.concatenate([top, total], axis=0)
+        half_stats[i] = level
         return carry
 
     lax.fori_loop(0, 2 * AUDIO_BLOCKS, cross_part, 0)
@@ -296,12 +298,9 @@
     def join_parts(i, carry):
         kind, b = lax.div(i, AUDIO_BLOCKS), lax.rem(i, AUDIO_BLOCKS)
         pair = lax.rem(me + kind * half, count)
-        mine = half_stats[i]
-        theirs = got_stats[(1 - kind) * AUDIO_BLOCKS + b]
-        top = jnp.maximum(mine[0:1], theirs[0:1])
-        weight = jnp.exp(mine[0:1] - top)
-        total = mine[1:2] * weight + theirs[1:2] * jnp.exp(theirs[0:1] - top)
-        found = half_found[i] * (weight / total)
+        above = got_stats[(1 - kind) * AUDIO_BLOCKS + b] - half_stats[i]
+        weight = jnp.where(above < 80.0, 1.0 / (1.0 + jnp.exp(jnp.minimum(above, 80.0))), 0.0)
+        found = half_found[i] * weight
         here = pl.ds(pl.multiple_of(b * block, block), block)
         part_audio[kind, here] = part_audio[kind, here] + gate(3, pair) * found.T
         return carry
@@ -417,16 +416,17 @@
 
     bf16, f32 = jnp.bfloat16, jnp.float32
     anywhere = pl.BlockSpec(memory_space=pl.ANY)
-    scalars = pl.BlockSpec(memory_space=pltpu.SMEM)
     video_out, audio_out = pl.pallas_call(
         functools.partial(exchange_and_attend, head_count),
         out_shape=(
             jax.ShapeDtypeStruct((count, video_rows, head_size), bf16),
             jax.ShapeDtypeStruct((clip_count, audio_rows, head_count, head_size), bf16),
         ),
-        in_specs=[scalars, scalars] + [anywhere] * 6,
+        in_specs=[pl.BlockSpec(memory_space=pltpu.SMEM)]
+        + [pl.BlockSpec(memory_space=pltpu.HBM)] * 7,
         out_specs=[anywhere] * 2,
         scratch_shapes=[
+            pltpu.SMEM(lengths.shape, lengths.dtype),
             pltpu.VMEM(gate_table.shape, f32),
             pltpu.VMEM((2, clip_count, 3, audio_rows, head_count, head_size), bf16),
             pltpu.VMEM((count, 6, quarters, HALF_TILE, head_size), bf16),
@@ -440,14 +440,13 @@
             pltpu.VMEM((count, video_rows, head_size), bf16),
             pltpu.VMEM((2, audio_total, head_size), f32),
             pltpu.VMEM((2 * AUDIO_BLOCKS, head_size, block), f32),
-            pltpu.VMEM((2 * AUDIO_BLOCKS, 2, block), f32),
-            pltpu.VMEM((2 * AUDIO_BLOCKS, 2, block), f32),
+            pltpu.VMEM((2 * AUDIO_BLOCKS, 1, block), f32),
+            pltpu.VMEM((2 * AUDIO_BLOCKS, 1, block), f32),
             pltpu.VMEM((2, count, quarters, HALF_TILE, head_size), bf16),
             pltpu.VMEM((2, 2, half, quarters, HALF_TILE, head_size), bf16),
             pltpu.VMEM((clip_count, audio_rows, head_count, head_size), bf16),
-            pltpu.SemaphoreType.REGULAR,
-            pltpu.SemaphoreType.REGULAR,
-            pltpu.SemaphoreType.DMA((3,)),
+            pltpu.SemaphoreType.REGULAR((int(math.log2(half)) - 1,)),
+            pltpu.SemaphoreType.DMA((4,)),
             pltpu.SemaphoreType.DMA((5,)),
             pltpu.SemaphoreType.DMA((5,)),
             pltpu.SemaphoreType.DMA,
@@ -456,17 +455,22 @@
             pltpu.SemaphoreType.DMA((2,)),
         ],
         compiler_params=pltpu.CompilerParams(
-            collective_id=0, has_side_effects=True, vmem_limit_bytes=62 * 2**20
+            collective_id=0, has_side_effects=True, vmem_limit_bytes=40 * 2**20
         ),
     )(
-        lengths,
         timestep,
-        gate_table,
-        video_self,
-        video_far,
-        video_far_halves,
-        heads_inside(audio_qkv),
-        heads_inside(audio_cross),
+        *(
+            pltpu.with_memory_space_constraint(tensor, pltpu.HBM)
+            for tensor in (
+                lengths,
+                gate_table,
+                video_self,
+                video_far,
+                video_far_halves,
+                heads_inside(audio_qkv),
+                heads_inside(audio_cross),
+            )
+        ),
     )
     return (
         video_out.reshape(clip_count, head_count, video_rows, head_size),

time: 593 us -> 591 us (level)
  no operation moved by 1% of the time
where the time goes in v4:
time: 591 us; the launch traced here: 586 us
  Pallas kernels  583 us (99%)
    pallas_call x1, Pallas kernels, on_device(): pl.pallas_call(functools.partial(exchange_and_attend, head_count), out_sh...  583 us

profile of v4, /device:TPU:37, one launch (start us, length us, event | category | flops | bytes accessed | tf_op | source)
XLA Modules:
  0.0 586.3 jit_solution(15903324024791294928)
XLA Ops:
  1.3 583.4 %shard_map.86 = (bf16[64,48,128]{2,1,0:T(8,128)(2,1)S(1)}, bf16[4,12,16,128]{3,2,1,0:T(8,128)(2,1)S(1)}) custom-call(s32[1]{0:T(128)S(6)} %copy.11.timestep, s32[2,4]{1,0:T(2,128)} %lengths_given.1, f32[50,4,16,128]{3,2,1,0:T(8,128)} %gate_table.1, bf16[64,3,48,128]{3,2,1,0:T(8,128)(2,1)} %bitcast.11, bf16[64,3,48,128]{3,2,1,0:T(8,128)(2,1)} %bitcast.9, ...), custom_call_target="tpu_custom_call" | custom-call | tf_op jit(solution)/shard_map/pallas_call | solution.py:419
  584.7 0.9 copy.12
  585.6 0.7 copy.13

commit v5 on v4

--- a/solution.py
+++ b/solution.py
@@ -12,6 +12,7 @@
 HALF_TILE = 4
 Q_DEVICES = 4
 AUDIO_BLOCKS = 3
+FIRST_REACH = 4
 
 
 def dot_rows(left, right):
@@ -122,7 +123,7 @@
     barrier = pltpu.get_barrier_semaphore()
 
     def greet(i, carry):
-        other = at_offset(lax.div(i, 2) - 1, lax.rem(i, 2))
+        other = at_offset(lax.div(i, 2) - FIRST_REACH, lax.rem(i, 2))
 
         @pl.when(other != me)
         def _():
@@ -130,8 +131,8 @@
 
         return carry
 
-    lax.fori_loop(0, 6, greet, 0)
-    pl.semaphore_wait(barrier, 5)
+    lax.fori_loop(0, 4 * FIRST_REACH + 2, greet, 0)
+    pl.semaphore_wait(barrier, 4 * FIRST_REACH + 1)
 
     def pass_on(step, distance):
         for offset in (-distance, distance):
@@ -170,7 +171,7 @@
         return carry
 
     quarter = chips // 4
-    reach, unsent = 1, half
+    reach, unsent = FIRST_REACH, half
     for step in range(known.shape[0]):
         pass_on(step, reach)
         start = max(0, 4 * (quarter - reach) - 2)
@@ -445,7 +446,7 @@
             pltpu.VMEM((2, count, quarters, HALF_TILE, head_size), bf16),
             pltpu.VMEM((2, 2, half, quarters, HALF_TILE, head_size), bf16),
             pltpu.VMEM((clip_count, audio_rows, head_count, head_size), bf16),
-            pltpu.SemaphoreType.REGULAR((int(math.log2(half)) - 1,)),
+            pltpu.SemaphoreType.REGULAR((int(math.log2(half // 2 // FIRST_REACH)),)),
             pltpu.SemaphoreType.DMA((4,)),
             pltpu.SemaphoreType.DMA((5,)),
             pltpu.SemaphoreType.DMA((5,)),

time: 591 us -> 589 us (level)
  no operation moved by 1% of the time
where the time goes in v5:
time: 589 us
  Pallas kernels  586 us (99%)
    pallas_call x1, Pallas kernels, on_device(): pl.pallas_call(functools.partial(exchange_and_attend, head_count), out_sh...  586 us

profile of v5, /device:TPU:37, one launch (start us, length us, event | category | flops | bytes accessed | tf_op | source)
XLA Modules:
  0.0 588.6 jit_solution(6216487803935655136)
XLA Ops:
  1.3 585.8 %shard_map.86 = (bf16[64,48,128]{2,1,0:T(8,128)(2,1)S(1)}, bf16[4,12,16,128]{3,2,1,0:T(8,128)(2,1)S(1)}) custom-call(s32[1]{0:T(128)S(6)} %copy.11.timestep, s32[2,4]{1,0:T(2,128)} %lengths_given.1, f32[50,4,16,128]{3,2,1,0:T(8,128)} %gate_table.1, bf16[64,3,48,128]{3,2,1,0:T(8,128)(2,1)} %bitcast.11, bf16[64,3,48,128]{3,2,1,0:T(8,128)(2,1)} %bitcast.9, ...), custom_call_target="tpu_custom_call" | custom-call | tf_op jit(solution)/shard_map/pallas_call | solution.py:420
  587.1 0.9 copy.12
  588.0 0.7 copy.13

commit v6 on v5

--- a/solution.py
+++ b/solution.py
@@ -12,7 +12,7 @@
 HALF_TILE = 4
 Q_DEVICES = 4
 AUDIO_BLOCKS = 3
-FIRST_REACH = 4
+FIRST_REACH = 2
 
 
 def dot_rows(left, right):

time: 589 us -> 593 us (level)
  no operation moved by 1% of the time
where the time goes in v6:
time: 593 us; the launch traced here: 591 us
  Pallas kernels  588 us (99%)
    pallas_call x1, Pallas kernels, on_device(): pl.pallas_call(functools.partial(exchange_and_attend, head_count), out_sh...  588 us

profile of v6, /device:TPU:37, one launch (start us, length us, event | category | flops | bytes accessed | tf_op | source)
XLA Modules:
  0.0 590.9 jit_solution(15861461313077297583)
XLA Ops:
  1.3 588.1 %shard_map.86 = (bf16[64,48,128]{2,1,0:T(8,128)(2,1)S(1)}, bf16[4,12,16,128]{3,2,1,0:T(8,128)(2,1)S(1)}) custom-call(s32[1]{0:T(128)S(6)} %copy.11.timestep, s32[2,4]{1,0:T(2,128)} %lengths_given.1, f32[50,4,16,128]{3,2,1,0:T(8,128)} %gate_table.1, bf16[64,3,48,128]{3,2,1,0:T(8,128)(2,1)} %bitcast.11, bf16[64,3,48,128]{3,2,1,0:T(8,128)(2,1)} %bitcast.9, ...), custom_call_target="tpu_custom_call" | custom-call | tf_op jit(solution)/shard_map/pallas_call | solution.py:420
  589.4 0.9 copy.12
  590.2 0.7 copy.13
